TPU v7x, 32 devices: a whole 2x2x4 slice. The times are simulated.
32 devices in a mesh: row: 8 (over z, y), col: 4 (over x, core).
Axes of the slice: x: 2, y: 2, z: 4, core: 2. Of those that a mesh axis runs over, the one named last changes fastest.
Arguments:
- params: float32 [4, 4096, 10240], P(None, ('row', 'col'))
- grads: bfloat16 [4, 4096, 10240], P(None, ('row', 'col')), may hold values from -6 to 6
- row_state_old: float32 [4, 4096], P(None, ('row', 'col')), may hold values from 0.05 to 0.5
- col_state_old: float32 [4, 10240], P(None, ('row', 'col')), may hold values from 0.05 to 0.5
- old_map: int32 [4, 32], replicated, may hold values from 0 to 31, each once within a row
- new_map: int32 [4, 32], replicated, may hold values from 0 to 31, each once within a row
Outputs:
- new_params: float32 [4, 4096, 10240], P(None, 'row', 'col')
- step_change: float32 [4, 4096, 10240], P(None, 'row', 'col')
- row_state: float32 [4, 4096], P(None, ('row', 'col'))
- col_state: float32 [4, 10240], P(None, ('row', 'col'))
Inputs may be any that keep to these rules, and one draw needn't show every extreme that they name: Each row of old_map is a permutation of 0 to 31. Each row of new_map is a permutation of 0 to 31.
All inputs are finite; a program needn't handle non-finite values.
Results may differ from a plain program's by a relative error of at most 0.0003.
Values may be sent and summed in bfloat16 or wider, within the bound.
No kernel may reach another device: no remote copies, remote signals or barrier semaphores. Data moves between devices by JAX's collectives and lax.ppermute only.
A program may use at most 192 MiB of HBM per device.

v0:
```python
import math
import jax
import jax.numpy as jnp
from jax import lax
from jax.sharding import PartitionSpec as P

D = 4096
FF = 10240
STEP = 4
eps_square = 1e-30
clip_limit = 1.0
highest = lax.Precision.HIGHEST


def reorder(stored, order, blocks):
    matrices = stored.shape[0]
    pieces = stored.reshape(matrices, blocks, stored.shape[1] // blocks)
    onehot = (order[:, :, None] == jnp.arange(blocks, dtype=jnp.int32)[None, None, :]).astype(
        jnp.float32
    )
    return jnp.einsum("mfb,mfw->mbw", onehot, pieces, precision=highest).reshape(matrices, -1)


def select_block(whole, order, blocks, flat_index):
    matrices = whole.shape[0]
    wanted = lax.dynamic_slice_in_dim(order, flat_index, 1, 1)
    onehot = (wanted == jnp.arange(blocks, dtype=jnp.int32)[None, :]).astype(jnp.float32)
    pieces = whole.reshape(matrices, blocks, whole.shape[1] // blocks)
    return jnp.einsum("mb,mbw->mw", onehot, pieces, precision=highest)


def totals(update_part, param_part):
    param_total = lax.psum(param_part, ("row", "col"))
    update_total = lax.psum(update_part, ("row", "col"))
    return (update_total, param_total)


def apply_update(weights, gradient, row_new, col_new, row_mean, step_rate):
    variance = row_new[:, :, None] * col_new[:, None, :] / row_mean[:, None, None]
    update = gradient / jnp.sqrt(variance)
    param_part = jnp.sum(weights * weights, axis=(1, 2))
    update_part = jnp.sum(update * update, axis=(1, 2))
    update_total, param_total = totals(update_part, param_part)
    count = weights.shape[0] * D * FF
    clip_factor = jnp.maximum(1.0, jnp.sqrt(jnp.sum(update_total) / count) / clip_limit)
    param_scale = jnp.sqrt(param_total / (D * FF) + 1e-06)
    change = -(step_rate * param_scale)[:, None, None] * update / clip_factor
    return (weights + change, change)


def shards(params, grads, row_state_old, col_state_old, old_map, new_map):
    decay_rate = 1.0 - float(STEP) ** (-0.8)
    step_rate = min(0.01, 1.0 / math.sqrt(STEP))
    row_count = lax.axis_size("row")
    col_count = lax.axis_size("col")
    blocks = row_count * col_count
    flat_index = lax.axis_index(("row", "col"))
    stored_rows, stored_cols = (
        lax.all_gather(row_state_old, ("row", "col"), axis=1, tiled=True),
        lax.all_gather(col_state_old, ("row", "col"), axis=1, tiled=True),
    )
    row_old = reorder(stored_rows, old_map, blocks)
    col_old = reorder(stored_cols, old_map, blocks)
    old_mean = jnp.mean(row_old, axis=1)
    weights = lax.all_to_all(params, "col", split_axis=2, concat_axis=1, tiled=True)
    moved = lax.all_to_all(grads, "col", split_axis=2, concat_axis=1, tiled=True)
    gradient = moved.astype(jnp.float32)
    squares = gradient * gradient + eps_square
    rows_here = gradient.shape[1]
    cols_here = gradient.shape[2]
    row_total = lax.psum(jnp.sum(squares, axis=2), "col")
    col_total, grand_total = lax.psum((jnp.sum(squares, axis=1), jnp.sum(row_total, axis=1)), "row")
    row_block = lax.dynamic_slice_in_dim(row_old, lax.axis_index("row") * rows_here, rows_here, 1)
    col_block = lax.dynamic_slice_in_dim(col_old, lax.axis_index("col") * cols_here, cols_here, 1)
    row_new = decay_rate * row_block + (1.0 - decay_rate) * row_total / FF
    col_new = decay_rate * col_block + (1.0 - decay_rate) * col_total / D
    row_mean = decay_rate * old_mean + (1.0 - decay_rate) * grand_total / (D * FF)
    new_params, step_change = apply_update(weights, gradient, row_new, col_new, row_mean, step_rate)
    whole_rows = lax.all_gather(row_new, "row", axis=1, tiled=True)
    whole_cols = lax.all_gather(col_new, "col", axis=1, tiled=True)
    row_state = select_block(whole_rows, new_map, blocks, flat_index)
    col_state = select_block(whole_cols, new_map, blocks, flat_index)
    return (new_params, step_change, row_state, col_state)


def solution(mesh):
    placed = (
        P(None, ("row", "col"), None),
        P(None, ("row", "col"), None),
        P(None, ("row", "col")),
        P(None, ("row", "col")),
        P(),
        P(),
    )
    return jax.shard_map(
        shards,
        mesh=mesh,
        in_specs=placed,
        out_specs=(
            P(None, "row", "col"),
            P(None, "row", "col"),
            P(None, ("row", "col")),
            P(None, ("row", "col")),
        ),
        check_vma=False,
    )
```

profile of v0, /device:TPU:0, one launch (start us, length us, event | category | flops | bytes accessed | tf_op | source)
XLA Modules:
  0.0 772.3 jit_solution(8924082937951834836)
XLA Ops:
  0.6 16.7 %copy.24 = bf16[4,128,10240]{1,0,2:T(4,128)(2,1)} copy(bf16[4,128,10240]{2,1,0:T(8,128)(2,1)} %param.7) | data formatting | bytes 20971520 | tf_op args[1]
  17.4 6.0 all-to-all-start.1
  23.4 23.8 %copy.22 = f32[4,128,10240]{1,0,2:T(4,128)} copy(f32[4,128,10240]{2,1,0:T(8,128)} %param.6) | data formatting | bytes 41943040 | tf_op args[0]
  47.2 92.4 %all-to-all-done.1 = bf16[4,128,10240]{1,0,2:T(4,128)(2,1)} async-done(((bf16[4,128,10240]{1,0,2:T(4,128)(2,1)}), bf16[4,128,10240]{1,0,2:T(4,128)(2,1)}, u32[]{:S(2)}, u32[]{:S(2)}) %all-to-all-start.1) | async-done | bytes 10485792 | tf_op jit(solution)/shard_map/all_to_all | solution.py:66
  139.6 7.7 all-to-all-start
  147.3 261.9 %all_gather.12 = f32[4,4096]{1,0:T(4,128)S(1)} all-gather(f32[4,128]{1,0:T(4,128)S(1)} %copy-done.4), channel_id=1, replica_groups=mesh['row'=8,'col'=4] {'row','col'}, dimensions={1}, use_global_device_ids=true | all-gather | bytes 67584 | tf_op jit(solution)/shard_map/all_gather | solution.py:59
  409.5 37.2 %all-gather = f32[32,320,4]{1,2,0:T(4,128)S(1)} all-gather(f32[1,320,4]{1,2,0:T(4,128)S(1)} %bitcast.64), channel_id=1, replica_groups=mesh['row'=8,'col'=4] {'row','col'}, dimensions={0}, use_global_device_ids=true | all-gather | bytes 168960 | tf_op jit(solution)/shard_map/all_gather | solution.py:60
  447.2 3.2 copy.34
  450.7 15.4 %fusion.2 = (f32[4,2560]{0,1:T(8,128)S(1)}, f32[4,4,128]{2,0,1:T(4,128)S(1)}) fusion(bf16[4,128,4,2560]{1,0,3,2:T(4,128)(2,1)} %bitcast.7), kind=kLoop, calls=%fused_computation.8 | loop fusion | flops 26202112 | bytes 10534912 | tf_op jit(solution)/shard_map/reduce_sum | solution.py:72
  466.1 7.4 psum.36
  473.6 73.3 %all-reduce.1 = (f32[4]{0:T(128)S(1)}, f32[4,2560]{0,1:T(8,128)S(1)}) all-reduce(f32[4]{0:T(128)S(1)} %get-tuple-element.13, f32[4,2560]{0,1:T(8,128)S(1)} %get-tuple-element.4), channel_id=1, replica_groups=mesh['row'=8,'col'=4] {'row'}, use_global_device_ids=true, to_apply=%region_8.0 | all-reduce | flops 10244 | bytes 81952 | tf_op jit(solution)/shard_map/psum | solution.py:72
  546.9 1.6 multiply_add_fusion.1
  548.9 32.1 %all_gather.15 = f32[4,10240]{0,1:T(8,128)} all-gather(f32[4,2560]{0,1:T(8,128)S(1)} %multiply_add_fusion.1), channel_id=1, replica_groups=mesh['row'=8,'col'=4] {'col'}, dimensions={1}, use_global_device_ids=true | all-gather | bytes 204800 | tf_op jit(solution)/shard_map/all_gather | solution.py:80
  581.0 3.6 copy.32
  585.4 11.3 %convert_bitcast_fusion = f32[4,4,128,2560]{2,0,3,1:T(4,128)} fusion(bf16[4,128,4,2560]{1,0,3,2:T(4,128)(2,1)} %bitcast.7), kind=kLoop, calls=%fused_computation | loop fusion | flops 5242880 | bytes 31457280 | tf_op jit(solution)/shard_map/convert_element_type | solution.py:67
  596.7 23.9 %copy.25 = f32[4,4,128,2560]{3,2,1,0:T(8,128)} copy(f32[4,4,128,2560]{2,0,3,1:T(4,128)} %convert_bitcast_fusion) | data formatting | bytes 41943040 | tf_op jit(solution)/shard_map/convert_element_type | solution.py:67
  620.6 30.5 %all_gather.14 = f32[4,4096]{1,0:T(4,128)S(1)} all-gather(f32[4,512]{1,0:T(4,128)S(1)} %get-tuple-element.12), channel_id=1, replica_groups=mesh['row'=8,'col'=4] {'row'}, dimensions={1}, use_global_device_ids=true | all-gather | bytes 73728 | tf_op jit(solution)/shard_map/all_gather | solution.py:79
  651.2 0.7 fusion.4
  651.9 13.1 %multiply_reduce_fusion = f32[4]{0:T(128)S(1)} fusion(bf16[4,128,4,2560]{1,0,3,2:T(4,128)(2,1)} %bitcast.7, f32[4]{0:T(128)S(1)} %multiply_add_fusion.3, f32[4,2560]{0,1:T(8,128)S(1)} %multiply_add_fusion.1, f32[4,4,128]{2,0,1:T(4,128)S(1)} %bitcast.61), kind=kLoop, calls=%fused_computation.5 | loop fusion | flops 31457276 | bytes 10534944 | tf_op jit(solution)/shard_map/reduce_sum | solution.py:42
  665.0 12.6 %multiply_reduce_fusion.1 = f32[4]{0:T(128)S(1)} fusion(f32[4,4,128,2560]{2,0,3,1:T(4,128)} %bitcast.1), kind=kLoop, calls=%fused_computation.7 | loop fusion | flops 10485756 | bytes 20971536 | tf_op jit(solution)/shard_map/reduce_sum | solution.py:41
  677.7 23.9 %copy.23 = f32[4,4,128,2560]{3,2,1,0:T(8,128)} copy(f32[4,4,128,2560]{2,0,3,1:T(4,128)} %bitcast.1) | data formatting | bytes 41943040 | tf_op jit(solution)/shard_map/all_to_all | solution.py:65
  701.6 39.7 %all-reduce = (f32[4]{0:T(128)S(1)}, f32[4]{0:T(128)S(1)}) all-reduce(f32[4]{0:T(128)S(1)} %multiply_reduce_fusion, f32[4]{0:T(128)S(1)} %multiply_reduce_fusion.1), channel_id=1, replica_groups=mesh['row'=8,'col'=4] {'row','col'}, use_global_device_ids=true, to_apply=%region_10.0 | all-reduce | flops 8 | bytes 64 | tf_op jit(solution)/shard_map/psum | solution.py:34
  741.3 0.6 reduce_sum.72
  742.7 29.6 %bitcast_add_fusion = (f32[4,512,2560]{2,1,0:T(8,128)}, f32[4,512,2560]{2,1,0:T(8,128)}) fusion(f32[4,4,128,2560]{3,2,1,0:T(8,128)} %copy.23, f32[]{:T(128)S(6)} %max.3, f32[4]{0:T(128)S(1)} %multiply_add_fusion.3, f32[4,2560]{1,0:T(4,128)S(1)} %copy.28, f32[4,512]{1,0:T(4,128)S(1)} %get-tuple-element.12, f32[4,4,128,2560]{3,2,1,0:T(8,128)} %copy.25, ...), kind=kLoop, calls=%fused_computation.4 | loop fusion | flops 31457280 | bytes 83935264 | tf_op jit(solution)/shard_map/add | solution.py:48
  (25 shorter events, 2.5 us)
Async XLA Ops:
  0.6 449.8 %copy-start = (s32[4,32]{1,0:T(4,128)S(1)}, s32[4,32]{1,0:T(4,128)}, u32[]{:S(2)}) copy-start(s32[4,32]{1,0:T(4,128)} %param.11) | copy-start | bytes 1540
  17.4 122.2 %all-to-all-start.1 = ((bf16[4,128,10240]{1,0,2:T(4,128)(2,1)}), bf16[4,128,10240]{1,0,2:T(4,128)(2,1)}, u32[]{:S(2)}, u32[]{:S(2)}) async-start(bf16[4,128,10240]{1,0,2:T(4,128)(2,1)} %copy.24), calls=%async_computation.1 | async-start | bytes 20971520 | tf_op jit(solution)/shard_map/all_to_all | solution.py:66
  47.2 100.2 %copy-start.4 = (f32[4,128]{1,0:T(4,128)S(1)}, f32[4,128]{1,0:T(4,128)}, u32[]{:S(2)}) copy-start(f32[4,128]{1,0:T(4,128)} %param.8) | copy-start | bytes 6148
  47.2 362.0 %copy-start.2 = (s32[4,32]{1,0:T(4,128)S(1)}, s32[4,32]{1,0:T(4,128)}, u32[]{:S(2)}) copy-start(s32[4,32]{1,0:T(4,128)} %param.10) | copy-start | bytes 1540
  47.2 362.3 %copy-start.3 = (f32[4,320]{1,0:T(4,128)S(1)}, f32[4,320]{1,0:T(4,128)}, u32[]{:S(2)}) copy-start(f32[4,320]{1,0:T(4,128)} %param.9) | copy-start | bytes 15364
  139.6 525.5 %all-to-all-start = ((f32[4,128,10240]{1,0,2:T(4,128)}), f32[4,128,10240]{1,0,2:T(4,128)}, u32[]{:S(2)}, u32[]{:S(2)}) async-start(f32[4,128,10240]{1,0,2:T(4,128)} %copy.22), calls=%async_computation | async-start | bytes 41943040 | tf_op jit(solution)/shard_map/all_to_all | solution.py:65
  742.6 29.6 %copy-start.1 = (s32[4,32]{1,0:T(4,128)S(1)}, s32[4,32]{1,0:T(4,128)}, u32[]{:S(2)}) copy-start(s32[4,32]{1,0:T(4,128)} %param.11) | copy-start | bytes 1540
where the time goes:
time: 775 us; the launch traced here: 772 us
  blocking collectives  482 us (62%)
  local copies, waits for them, and re-layouts  96.7 us (12%)
  waiting for transfers between devices  92.4 us (12%)
  other arithmetic  84.5 us (11%)
  starting transfers between devices  13.7 us (2%)
    all_gather x1, blocking collectives, shards(): lax.all_gather(row_state_old, ('row', 'col'), axis=1, tiled=True)  262 us
    all_to_all x1, waiting for transfers between devices, shards(): lax.all_to_all(grads, 'col', split_axis=2, concat_axis=1, tiled=True)  92.4 us
    psum x1, blocking collectives, shards(): lax.psum((jnp.sum(squares, axis=1), jnp.sum(row_total, axis=1)), 'row')  73.3 us
    unnamed x14, local copies, waits for them, and re-layouts  40.7 us
    psum x1, blocking collectives, totals(): update_total = lax.psum(update_part, ('row', 'col'))  39.7 us
    all_gather x1, blocking collectives, shards(): lax.all_gather(col_state_old, ('row', 'col'), axis=1, tiled=True)  37.2 us
    all_gather x1, blocking collectives, shards(): whole_cols = lax.all_gather(col_new, 'col', axis=1, tiled=True)  32.1 us
    all_gather x1, blocking collectives, shards(): whole_rows = lax.all_gather(row_new, 'row', axis=1, tiled=True)  30.5 us
  transfers between devices with their start and end apart: 2, of which 1 were waited for; matrix products, arithmetic and copies ran while one was open for 13% of the time, Pallas kernels for 0%

commit v1 on v0

--- a/solution.py
+++ b/solution.py
@@ -63,7 +63,15 @@
     col_old = reorder(stored_cols, old_map, blocks)
     old_mean = jnp.mean(row_old, axis=1)
     weights = lax.all_to_all(params, "col", split_axis=2, concat_axis=1, tiled=True)
-    moved = lax.all_to_all(grads, "col", split_axis=2, concat_axis=1, tiled=True)
+    moved = jnp.concatenate(
+        jax.lax.all_to_all(
+            jnp.stack(jnp.split(grads, jax.lax.axis_size("col"), axis=2)),
+            "col",
+            split_axis=0,
+            concat_axis=0,
+        ),
+        axis=1,
+    )
     gradient = moved.astype(jnp.float32)
     squares = gradient * gradient + eps_square
     rows_here = gradient.shape[1]

time: 775 us -> 675 us (0.87)
  blocking collectives: 482 us -> 413 us
  local copies, waits for them, and re-layouts: 96.7 us -> 70.2 us
    psum x1, blocking collectives: 73.3 us -> 33.8 us  [shards(): lax.psum((jnp.sum(squares, axis=1), jnp.sum(row_total, axis=1)), 'row')]
    all_gather x1, blocking collectives: 32.1 us -> 5.51 us  [shards(): whole_cols = lax.all_gather(col_new, 'col', axis=1, tiled=True)]
    unnamed x14 -> x13, local copies, waits for them, and re-layouts: 40.7 us -> 24 us
  transfers between devices with their start and end apart: 2 -> 2, of which waited for: 1 -> 1; matrix products, arithmetic and copies ran while one was open for 13% -> 11% of each run, Pallas kernels for 0% -> 0%
where the time goes in v1:
time: 675 us; the launch traced here: 673 us
  blocking collectives  413 us (61%)
  waiting for transfers between devices  92.4 us (14%)
  other arithmetic  80.4 us (12%)
  local copies, waits for them, and re-layouts  70.2 us (10%)
  starting transfers between devices  13.7 us (2%)
    all_gather x1, blocking collectives, shards(): lax.all_gather(row_state_old, ('row', 'col'), axis=1, tiled=True)  262 us
    all_to_all x1, waiting for transfers between devices, shards(): jax.lax.all_to_all(jnp.stack(jnp.split(grads, jax.lax.axis_size('col'), a...  92.4 us
    all_gather x1, blocking collectives, shards(): lax.all_gather(col_state_old, ('row', 'col'), axis=1, tiled=True)  37.2 us
    psum x1, blocking collectives, totals(): update_total = lax.psum(update_part, ('row', 'col'))  36.8 us
    psum x1, blocking collectives, shards(): lax.psum((jnp.sum(squares, axis=1), jnp.sum(row_total, axis=1)), 'row')  33.8 us
    all_gather x1, blocking collectives, shards(): whole_rows = lax.all_gather(row_new, 'row', axis=1, tiled=True)  30.7 us
    add x1, other arithmetic, apply_update(): return (weights + change, change)  29.6 us
    unnamed x13, local copies, waits for them, and re-layouts  24 us
  transfers between devices with their start and end apart: 2, of which 1 were waited for; matrix products, arithmetic and copies ran while one was open for 11% of the time, Pallas kernels for 0%

profile of v1, /device:TPU:0, one launch (start us, length us, event | category | flops | bytes accessed | tf_op | source)
XLA Modules:
  0.0 672.9 jit_solution(4162792593633012166)
XLA Ops:
  0.6 4.6 slice_bitcast_fusion.3
  5.2 4.8 pad_maximum_fusion
  10.0 6.0 all-to-all-start.1
  16.0 23.8 %copy.17 = f32[4,128,10240]{1,0,2:T(4,128)} copy(f32[4,128,10240]{2,1,0:T(8,128)} %param.6) | data formatting | bytes 41943040 | tf_op args[0]
  39.8 92.4 %all-to-all-done.1 = bf16[4,4,128,2560]{3,2,1,0:T(8,128)(2,1)} async-done(((bf16[4,4,128,2560]{3,2,1,0:T(8,128)(2,1)}), bf16[4,4,128,2560]{3,2,1,0:T(8,128)(2,1)}, u32[]{:S(2)}, u32[]{:S(2)}) %all-to-all-start.1) | async-done | bytes 10485792 | tf_op jit(solution)/shard_map/all_to_all | solution.py:67
  132.2 7.7 %all-to-all-start = ((f32[4,128,10240]{1,0,2:T(4,128)}), f32[4,128,10240]{1,0,2:T(4,128)}, u32[]{:S(2)}, u32[]{:S(2)}) async-start(f32[4,128,10240]{1,0,2:T(4,128)} %copy.17), calls=%async_computation | async-start | bytes 41943040 | tf_op jit(solution)/shard_map/all_to_all | solution.py:65
  140.0 261.9 %all_gather.12 = f32[4,4096]{1,0:T(4,128)S(1)} all-gather(f32[4,128]{1,0:T(4,128)S(1)} %copy-done.4), channel_id=1, replica_groups=mesh['row'=8,'col'=4] {'row','col'}, dimensions={1}, use_global_device_ids=true | all-gather | bytes 67584 | tf_op jit(solution)/shard_map/all_gather | solution.py:59
  401.8 0.3 fusion.18
  402.2 37.2 %all-gather = f32[32,320,4]{1,2,0:T(4,128)S(1)} all-gather(f32[1,320,4]{1,2,0:T(4,128)S(1)} %bitcast.66), channel_id=1, replica_groups=mesh['row'=8,'col'=4] {'row','col'}, dimensions={0}, use_global_device_ids=true | all-gather | bytes 168960 | tf_op jit(solution)/shard_map/all_gather | solution.py:60
  440.3 9.4 %fusion.2 = (f32[4,2560]{1,0:T(4,128)S(1)}, f32[4,4,128]{2,0,1:T(4,128)S(1)}) fusion(bf16[4,4,128,2560]{3,2,1,0:T(8,128)(2,1)} %all-to-all-done.1), kind=kLoop, calls=%fused_computation.8 | loop fusion | flops 26202112 | bytes 10534912 | tf_op jit(solution)/shard_map/reduce_sum | solution.py:80
  449.7 7.4 %psum.36 = f32[4,512]{1,0:T(4,128)S(1)} all-reduce(f32[4,512]{1,0:T(4,128)S(1)} %bitcast.65), channel_id=1, replica_groups=mesh['row'=8,'col'=4] {'col'}, use_global_device_ids=true, to_apply=%region_3.0 | all-reduce | flops 2048 | bytes 16384 | tf_op jit(solution)/shard_map/psum | solution.py:79
  457.3 33.8 %all-reduce.1 = (f32[4]{0:T(128)S(1)}, f32[4,2560]{1,0:T(4,128)S(1)}) all-reduce(f32[4]{0:T(128)S(1)} %get-tuple-element.17, f32[4,2560]{1,0:T(4,128)S(1)} %get-tuple-element.4), channel_id=1, replica_groups=mesh['row'=8,'col'=4] {'row'}, use_global_device_ids=true, to_apply=%region_8.0 | all-reduce | flops 10244 | bytes 81952 | tf_op jit(solution)/shard_map/psum | solution.py:80
  491.1 14.5 %convert_bitcast_fusion = f32[4,4,128,2560]{3,2,0,1:T(8,128)} fusion(bf16[4,4,128,2560]{3,2,1,0:T(8,128)(2,1)} %all-to-all-done.1), kind=kLoop, calls=%fused_computation.4 | loop fusion | flops 5242880 | bytes 31457280 | tf_op jit(solution)/shard_map/convert_element_type | solution.py:75
  505.6 16.5 %copy.19 = f32[4,4,128,2560]{3,2,1,0:T(8,128)} copy(f32[4,4,128,2560]{3,2,0,1:T(8,128)} %convert_bitcast_fusion) | data formatting | bytes 41943040 | tf_op jit(solution)/shard_map/convert_element_type | solution.py:75
  522.1 5.5 all_gather.15
  527.9 0.6 copy.45
  528.5 30.7 %all_gather.14 = f32[4,4096]{1,0:T(4,128)S(1)} all-gather(f32[4,512]{1,0:T(4,128)S(1)} %get-tuple-element.16), channel_id=1, replica_groups=mesh['row'=8,'col'=4] {'row'}, dimensions={1}, use_global_device_ids=true | all-gather | bytes 73728 | tf_op jit(solution)/shard_map/all_gather | solution.py:87
  559.2 0.7 fusion.4
  560.0 8.7 %multiply_reduce_fusion = f32[4]{0:T(128)S(1)} fusion(bf16[4,4,128,2560]{3,2,1,0:T(8,128)(2,1)} %all-to-all-done.1, f32[4]{0:T(128)S(1)} %multiply_add_fusion.3, f32[4,2560]{1,0:T(4,128)S(1)} %multiply_add_fusion.1, f32[4,4,128]{2,0,1:T(4,128)S(1)} %bitcast.63), kind=kLoop, calls=%fused_computation.5 | loop fusion | flops 31457276 | bytes 10534944 | tf_op jit(solution)/shard_map/reduce_sum | solution.py:42
  568.6 12.6 %multiply_reduce_fusion.1 = f32[4]{0:T(128)S(1)} fusion(f32[4,4,128,2560]{2,0,3,1:T(4,128)} %bitcast.1), kind=kLoop, calls=%fused_computation.7 | loop fusion | flops 10485756 | bytes 20971536 | tf_op jit(solution)/shard_map/reduce_sum | solution.py:41
  581.3 23.9 %copy.18 = f32[4,4,128,2560]{3,2,1,0:T(8,128)} copy(f32[4,4,128,2560]{2,0,3,1:T(4,128)} %bitcast.1) | data formatting | bytes 41943040 | tf_op jit(solution)/shard_map/all_to_all | solution.py:65
  605.2 36.8 %all-reduce = (f32[4]{0:T(128)S(1)}, f32[4]{0:T(128)S(1)}) all-reduce(f32[4]{0:T(128)S(1)} %multiply_reduce_fusion, f32[4]{0:T(128)S(1)} %multiply_reduce_fusion.1), channel_id=1, replica_groups=mesh['row'=8,'col'=4] {'row','col'}, use_global_device_ids=true, to_apply=%region_10.0 | all-reduce | flops 8 | bytes 64 | tf_op jit(solution)/shard_map/psum | solution.py:34
  642.0 0.6 reduce_sum.72
  643.3 29.6 %bitcast_add_fusion = (f32[4,512,2560]{2,1,0:T(8,128)}, f32[4,512,2560]{2,1,0:T(8,128)}) fusion(f32[4,4,128,2560]{3,2,1,0:T(8,128)} %copy.18, f32[]{:T(128)S(6)} %max.3, f32[4]{0:T(128)S(1)} %multiply_add_fusion.3, f32[4,2560]{1,0:T(4,128)S(1)} %multiply_add_fusion.1, f32[4,512]{1,0:T(4,128)S(1)} %get-tuple-element.16, f32[4,4,128,2560]{3,2,1,0:T(8,128)} %copy.19, ...), kind=kLoop, calls=%fused_computation.3 | loop fusion | flops 31457280 | bytes 83935264 | tf_op jit(solution)/shard_map/add | solution.py:48
  (25 shorter events, 1.5 us)
Async XLA Ops:
  0.6 439.4 %copy-start = (s32[4,32]{1,0:T(4,128)S(1)}, s32[4,32]{1,0:T(4,128)}, u32[]{:S(2)}) copy-start(s32[4,32]{1,0:T(4,128)} %param.11) | copy-start | bytes 1540
  10.0 122.2 %all-to-all-start.1 = ((bf16[4,4,128,2560]{3,2,1,0:T(8,128)(2,1)}), bf16[4,4,128,2560]{3,2,1,0:T(8,128)(2,1)}, u32[]{:S(2)}, u32[]{:S(2)}) async-start(bf16[4,4,128,2560]{3,2,1,0:T(8,128)(2,1)} %pad_maximum_fusion), calls=%async_computation.1 | async-start | bytes 20971520 | tf_op jit(solution)/shard_map/all_to_all | solution.py:67
  39.8 100.1 %copy-start.4 = (f32[4,128]{1,0:T(4,128)S(1)}, f32[4,128]{1,0:T(4,128)}, u32[]{:S(2)}) copy-start(f32[4,128]{1,0:T(4,128)} %param.8) | copy-start | bytes 6148
  39.8 362.0 %copy-start.2 = (s32[4,32]{1,0:T(4,128)S(1)}, s32[4,32]{1,0:T(4,128)}, u32[]{:S(2)}) copy-start(s32[4,32]{1,0:T(4,128)} %param.10) | copy-start | bytes 1540
  39.8 362.3 %copy-start.3 = (f32[4,320]{1,0:T(4,128)S(1)}, f32[4,320]{1,0:T(4,128)}, u32[]{:S(2)}) copy-start(f32[4,320]{1,0:T(4,128)} %param.9) | copy-start | bytes 15364
  132.2 436.4 %all-to-all-start = ((f32[4,128,10240]{1,0,2:T(4,128)}), f32[4,128,10240]{1,0,2:T(4,128)}, u32[]{:S(2)}, u32[]{:S(2)}) async-start(f32[4,128,10240]{1,0,2:T(4,128)} %copy.17), calls=%async_computation | async-start | bytes 41943040 | tf_op jit(solution)/shard_map/all_to_all | solution.py:65
  643.3 29.6 %copy-start.1 = (s32[4,32]{1,0:T(4,128)S(1)}, s32[4,32]{1,0:T(4,128)}, u32[]{:S(2)}) copy-start(s32[4,32]{1,0:T(4,128)} %param.11) | copy-start | bytes 1540
